TPU v7x, 32 devices: a whole 2x2x4 slice. The times are simulated.
32 devices in a mesh: row: 2 (over y), col: 4 (over x, core), rep: 4 (over z).
Axes of the slice: x: 2, y: 2, z: 4, core: 2. Of those that a mesh axis runs over, the one named last changes fastest.
Arguments:
- hidden: bfloat16 [512, 7168], P('rep'), may hold values from -6 to 6
- train_weight: bfloat16 [7168, 16384], P(('rep', 'row'), 'col'), may hold values from -0.0625 to 0.0625
- shard_order: int32 [4, 4, 2], replicated, may hold values from 0 to 1, each once within a row
Outputs:
- served_weight: bfloat16 [7168, 16384], P(None, ('col', 'row'))
- projected: float32 [512, 16384], P('rep', ('col', 'row'))
Inputs may be any that keep to these rules, and one draw needn't show every extreme that they name: Each shard_order[c, k] is a permutation of 0 to 1.
All inputs are finite; a program needn't handle non-finite values.
Results may differ from a plain program's by a relative error of at most 0.001.
Values may be sent and summed in bfloat16 or wider, within the bound.
A program may use at most 128 MiB of HBM per device.

v0:
```python
import jax
import jax.numpy as jnp
from jax import lax
from jax.sharding import PartitionSpec as P


def shards(hidden, train_weight, shard_order):
    row_count = lax.axis_size("row")
    rows_tile = train_weight.shape[0]
    cols_tile = train_weight.shape[1]
    piece_cols = cols_tile // row_count
    sub_count = shard_order.shape[1]
    sub_cols = piece_cols // sub_count
    my_order = lax.dynamic_index_in_dim(shard_order, lax.axis_index("col"), 0, keepdims=False)
    source_ids = lax.broadcasted_iota(jnp.int32, (sub_count, row_count, row_count), 2)
    selector = (my_order[:, :, None] == source_ids).astype(jnp.bfloat16)
    tiled = train_weight.reshape(rows_tile, row_count, sub_count, sub_cols)
    picked = jnp.einsum("ksj,rjkc->rskc", selector, tiled, preferred_element_type=jnp.float32)
    ordered = picked.astype(jnp.bfloat16).reshape(rows_tile, cols_tile)
    column = lax.all_to_all(ordered, "row", split_axis=1, concat_axis=0, tiled=True)
    served = lax.all_gather(column, "rep", axis=0, tiled=True)
    projected = jnp.dot(hidden, served, preferred_element_type=jnp.float32)
    return (served, projected)


def solution(mesh):
    placed = (P("rep", None), P(("rep", "row"), "col"), P())
    return jax.shard_map(
        shards,
        mesh=mesh,
        in_specs=placed,
        out_specs=(P(None, ("col", "row")), P("rep", ("col", "row"))),
        check_vma=False,
    )
```

profile of v0, /device:TPU:0, one launch (start us, length us, event | category | flops | bytes accessed | tf_op | source)
XLA Modules:
  0.0 697.5 jit_solution(17215963833131791758)
XLA Ops:
  7.2 0.0 copy-start
  7.2 0.0 all-gather.2.cloned.1.call-start
  7.2 0.8 dynamic-slice_bitcast_fusion
  8.0 0.1 copy.12
  8.1 12.8 %reshape.14 = bf16[896,2,4,512]{3,2,1,0:T(4,128)(2,1)} reshape(bf16[896,4096]{1,0:T(8,128)(2,1)} %param.4) | data formatting | bytes 14680064 | tf_op jit(solution)/shard_map/reshape | solution.py:17
  21.0 18.4 %fusion = bf16[896,2,4,512]{3,1,0,2:T(2,128)(2,1)} fusion(bf16[896,2,4,512]{3,2,1,0:T(4,128)(2,1)} %reshape.14, s32[4,2]{1,0:T(4,128)S(1)} %copy.12), kind=kOutput, calls=%fused_computation.1 | convolution fusion | flops 18350096 | bytes 14680096 | tf_op jit(solution)/shard_map/ksj,rjkc->rskc/dot_general | solution.py:18
  39.3 18.6 %copy.14 = bf16[896,2,4,512]{0,3,2,1:T(8,128)(2,1)} copy(bf16[896,2,4,512]{3,1,0,2:T(2,128)(2,1)} %fusion) | data formatting | bytes 14680064 | tf_op jit(solution)/shard_map/convert_element_type | solution.py:19
  57.9 92.8 %all_to_all.19 = bf16[896,2,2048]{0,2,1:T(8,128)(2,1)} all-to-all(bf16[896,2,2048]{0,2,1:T(8,128)(2,1)} %bitcast.17), channel_id=1, replica_groups=mesh['row'=2,'col'=4,'rep'=4] {'row'}, dimensions={1} | all-to-all | bytes 14680064 | tf_op jit(solution)/shard_map/all_to_all | solution.py:20
  150.8 11.3 %copy.15 = bf16[2,896,2048]{2,1,0:T(8,128)(2,1)} copy(bf16[2,896,2048]{1,2,0:T(8,128)(2,1)} %bitcast.18) | data formatting | bytes 14680064 | tf_op jit(solution)/shard_map/all_to_all | solution.py:20
  162.0 0.0 all-gather.2.cloned.1.call-update
  162.1 493.7 %all-gather.2.cloned.1.call-done = bf16[7168,2048]{1,0:T(8,128)(2,1)} async-done(((bf16[1792,2048]{1,0:T(8,128)(2,1)}), bf16[7168,2048]{1,0:T(8,128)(2,1)}) %all-gather.2.cloned.1.call-update) | async-done | bytes 29360144 | tf_op jit(solution)/shard_map/all_gather | solution.py:21
  655.8 0.0 copy-done
  655.8 13.3 %convolution_bitcast_fusion = f32[128,2048]{0,1:T(8,128)S(1)} fusion(bf16[7168,2048]{1,0:T(8,128)(2,1)} %all-gather.2.cloned.1.call-done, bf16[128,7168]{1,0:T(8,128)(2,1)S(1)} %copy-done), kind=kOutput, calls=%fused_computation.3 | convolution fusion | flops 3758096384 | bytes 32243712 | tf_op jit(solution)/shard_map/dot_general | solution.py:22
  669.1 1.3 copy.16
  670.4 0.0 copy-start.1
  670.4 20.2 %copy.21 = bf16[7168,2048]{1,0:T(8,128)(2,1)} copy(bf16[7168,2048]{1,0:T(8,128)(2,1)} %all-gather.2.cloned.1.call-done) | data formatting | bytes 58720256
  690.6 0.0 copy-done.1
Async XLA Ops:
  7.2 648.6 %copy-start = (bf16[128,7168]{1,0:T(8,128)(2,1)S(1)}, bf16[128,7168]{1,0:T(8,128)(2,1)}, u32[]{:S(2)}) copy-start(bf16[128,7168]{1,0:T(8,128)(2,1)} %param.3) | copy-start | bytes 5505028
  7.2 648.6 %all-gather.2.cloned.1.call-start = ((), (), s32[]{:S(2)}) async-start(), calls=%async_computation.1 | async-start | bytes 36700160 | tf_op jit(solution)/shard_map/all_gather | solution.py:21
  670.4 20.2 %copy-start.1 = (bf16[128,7168]{1,0:T(8,128)(2,1)S(1)}, bf16[128,7168]{1,0:T(8,128)(2,1)}, u32[]{:S(2)}) copy-start(bf16[128,7168]{1,0:T(8,128)(2,1)} %param.3) | copy-start | bytes 5505028
Sparse Core Ops, SparseCore 0:
  162.2 493.5 all-gather.1
where the time goes:
time: 699 us; the launch traced here: 697 us
  waiting for transfers between devices  494 us (71%)
  blocking collectives  92.8 us (13%)
  local copies, waits for them, and re-layouts  65.1 us (9%)
  matrix products  31.7 us (5%)
  between operations  14.1 us (2%)
    all_gather x1, waiting for transfers between devices, shards(): served = lax.all_gather(column, 'rep', axis=0, tiled=True)  494 us
    all_to_all x1, blocking collectives, shards(): lax.all_to_all(ordered, 'row', split_axis=1, concat_axis=0, tiled=True)  92.8 us
    unnamed x6, local copies, waits for them, and re-layouts  21.5 us
    convert_element_type x1, local copies, waits for them, and re-layouts, shards(): ordered = picked.astype(jnp.bfloat16).reshape(rows_tile, cols_tile)  18.6 us
    dot_general x1, matrix products, shards(): jnp.einsum('ksj,rjkc->rskc', selector, tiled, preferred_element_type=jnp....  18.4 us
  transfers between devices with their start and end apart: 1, of which 1 were waited for; matrix products, arithmetic and copies ran while one was open for 0% of the time, Pallas kernels for 0%

commit v1 on v0

--- a/solution.py
+++ b/solution.py
@@ -5,6 +5,18 @@
 
 
 def shards(hidden, train_weight, shard_order):
+
+    def save_the_layers_all(x0, peer_axis):
+        return jnp.concatenate(
+            lax.all_to_all(
+                jnp.stack(jnp.split(x0, lax.psum(1, peer_axis), axis=1)),
+                peer_axis,
+                concat_axis=0,
+                split_axis=0,
+            ),
+            axis=0,
+        )
+
     row_count = lax.axis_size("row")
     rows_tile = train_weight.shape[0]
     cols_tile = train_weight.shape[1]
@@ -17,7 +29,7 @@
     tiled = train_weight.reshape(rows_tile, row_count, sub_count, sub_cols)
     picked = jnp.einsum("ksj,rjkc->rskc", selector, tiled, preferred_element_type=jnp.float32)
     ordered = picked.astype(jnp.bfloat16).reshape(rows_tile, cols_tile)
-    column = lax.all_to_all(ordered, "row", split_axis=1, concat_axis=0, tiled=True)
+    column = save_the_layers_all(ordered, "row")
     served = lax.all_gather(column, "rep", axis=0, tiled=True)
     projected = jnp.dot(hidden, served, preferred_element_type=jnp.float32)
     return (served, projected)

time: 699 us -> 701 us (level)
  no operation moved by 1% of the time
where the time goes in v1:
time: 701 us; the launch traced here: 700 us
  waiting for transfers between devices  494 us (70%)
  blocking collectives  86.8 us (12%)
  local copies, waits for them, and re-layouts  70.7 us (10%)
  matrix products  31.7 us (5%)
  between operations  14.1 us (2%)
    all_gather x1, waiting for transfers between devices, shards(): served = lax.all_gather(column, 'rep', axis=0, tiled=True)  494 us
    all_to_all x1, blocking collectives, save_the_layers_all(): lax.all_to_all(jnp.stack(jnp.split(x0, lax.psum(1, peer_axis), axis=1)),...  86.8 us
    unnamed x6, local copies, waits for them, and re-layouts  21.5 us
    convert_element_type x1, local copies, waits for them, and re-layouts, shards(): ordered = picked.astype(jnp.bfloat16).reshape(rows_tile, cols_tile)  18.6 us
    dot_general x1, matrix products, shards(): jnp.einsum('ksj,rjkc->rskc', selector, tiled, preferred_element_type=jnp....  18.4 us
  transfers between devices with their start and end apart: 1, of which 1 were waited for; matrix products, arithmetic and copies ran while one was open for 0% of the time, Pallas kernels for 0%

profile of v1, /device:TPU:0, one launch (start us, length us, event | category | flops | bytes accessed | tf_op | source)
XLA Modules:
  0.0 699.8 jit_solution(5270363923930004330)
XLA Ops:
  7.2 0.0 copy-start
  7.2 0.0 all-gather.2.cloned.1.call-start
  7.2 0.8 dynamic-slice_bitcast_fusion
  8.0 0.1 copy.12
  8.1 12.8 %reshape.15 = bf16[896,2,4,512]{3,2,1,0:T(4,128)(2,1)} reshape(bf16[896,4096]{1,0:T(8,128)(2,1)} %param.4) | data formatting | bytes 14680064 | tf_op jit(solution)/shard_map/reshape | solution.py:29
  21.0 18.4 %fusion = bf16[896,2,4,512]{3,1,0,2:T(2,128)(2,1)} fusion(bf16[896,2,4,512]{3,2,1,0:T(4,128)(2,1)} %reshape.15, s32[4,2]{1,0:T(4,128)S(1)} %copy.12), kind=kOutput, calls=%fused_computation.1 | convolution fusion | flops 18350096 | bytes 14680096 | tf_op jit(solution)/shard_map/ksj,rjkc->rskc/dot_general | solution.py:30
  39.3 18.6 %copy.14 = bf16[896,2,4,512]{0,3,2,1:T(8,128)(2,1)} copy(bf16[896,2,4,512]{3,1,0,2:T(2,128)(2,1)} %fusion) | data formatting | bytes 14680064 | tf_op jit(solution)/shard_map/convert_element_type | solution.py:31
  57.9 5.5 slice_bitcast_fusion.1
  63.5 2.8 pad_maximum_fusion
  66.2 86.8 %all_to_all.5 = bf16[2,896,2048]{1,2,0:T(8,128)(2,1)} all-to-all(bf16[2,896,2048]{1,2,0:T(8,128)(2,1)S(1)} %pad_maximum_fusion), channel_id=1, replica_groups=mesh['row'=2,'col'=4,'rep'=4] {'row'}, dimensions={0} | all-to-all | bytes 14680064 | tf_op jit(solution)/shard_map/all_to_all | solution.py:11
  153.1 11.3 %copy.15 = bf16[2,896,2048]{2,1,0:T(8,128)(2,1)} copy(bf16[2,896,2048]{1,2,0:T(8,128)(2,1)} %all_to_all.5) | data formatting | bytes 14680064 | tf_op jit(solution)/shard_map/all_to_all | solution.py:11
  164.3 0.0 all-gather.2.cloned.1.call-update
  164.3 493.7 %all-gather.2.cloned.1.call-done = bf16[7168,2048]{1,0:T(8,128)(2,1)} async-done(((bf16[1792,2048]{1,0:T(8,128)(2,1)}), bf16[7168,2048]{1,0:T(8,128)(2,1)}) %all-gather.2.cloned.1.call-update) | async-done | bytes 29360144 | tf_op jit(solution)/shard_map/all_gather | solution.py:33
  658.1 0.0 copy-done
  658.1 13.3 %convolution_bitcast_fusion = f32[128,2048]{0,1:T(8,128)S(1)} fusion(bf16[7168,2048]{1,0:T(8,128)(2,1)} %all-gather.2.cloned.1.call-done, bf16[128,7168]{1,0:T(8,128)(2,1)S(1)} %copy-done), kind=kOutput, calls=%fused_computation.6 | convolution fusion | flops 3758096384 | bytes 32243712 | tf_op jit(solution)/shard_map/dot_general | solution.py:34
  671.4 1.3 copy.16
  672.7 0.0 copy-start.1
  672.7 20.2 %copy.21 = bf16[7168,2048]{1,0:T(8,128)(2,1)} copy(bf16[7168,2048]{1,0:T(8,128)(2,1)} %all-gather.2.cloned.1.call-done) | data formatting | bytes 58720256
  692.9 0.0 copy-done.1
Async XLA Ops:
  7.2 650.9 %copy-start = (bf16[128,7168]{1,0:T(8,128)(2,1)S(1)}, bf16[128,7168]{1,0:T(8,128)(2,1)}, u32[]{:S(2)}) copy-start(bf16[128,7168]{1,0:T(8,128)(2,1)} %param.3) | copy-start | bytes 5505028
  7.2 650.9 %all-gather.2.cloned.1.call-start = ((), (), s32[]{:S(2)}) async-start(), calls=%async_computation.1 | async-start | bytes 36700160 | tf_op jit(solution)/shard_map/all_gather | solution.py:33
  672.7 20.2 %copy-start.1 = (bf16[128,7168]{1,0:T(8,128)(2,1)S(1)}, bf16[128,7168]{1,0:T(8,128)(2,1)}, u32[]{:S(2)}) copy-start(bf16[128,7168]{1,0:T(8,128)(2,1)} %param.3) | copy-start | bytes 5505028
Sparse Core Ops, SparseCore 0:
  164.5 493.5 all-gather.1

commit v2 on v0

--- a/solution.py
+++ b/solution.py
@@ -5,6 +5,25 @@
 
 
 def shards(hidden, train_weight, shard_order):
+
+    def test_leaves_over_axis(matrix):
+        axis_id = "rep"
+        nd = lax.axis_size(axis_id)
+        frames = tuple(((t, (t + 1) % nd) for t in range(nd)))
+
+        def turn_the_leaf(new):
+            if len(new) == nd:
+                return new
+            t_next = turn_the_leaf([lax.ppermute(new[0], axis_name=axis_id, perm=frames), *new])
+            return t_next
+
+        before = jnp.roll(
+            jnp.concatenate(turn_the_leaf([matrix]), 0),
+            (lax.axis_index(axis_id) + 1) * matrix.shape[0],
+            0,
+        )
+        return before
+
     row_count = lax.axis_size("row")
     rows_tile = train_weight.shape[0]
     cols_tile = train_weight.shape[1]
@@ -18,7 +37,7 @@
     picked = jnp.einsum("ksj,rjkc->rskc", selector, tiled, preferred_element_type=jnp.float32)
     ordered = picked.astype(jnp.bfloat16).reshape(rows_tile, cols_tile)
     column = lax.all_to_all(ordered, "row", split_axis=1, concat_axis=0, tiled=True)
-    served = lax.all_gather(column, "rep", axis=0, tiled=True)
+    served = test_leaves_over_axis(column)
     projected = jnp.dot(hidden, served, preferred_element_type=jnp.float32)
     return (served, projected)
 

time: 699 us -> 729 us (1.043)
  local copies, waits for them, and re-layouts: 65.1 us -> 122 us
  waiting for transfers between devices: 494 us -> 479 us
  between operations: 14.1 us -> 0.67 us
    all_gather x1 -> x0, waiting for transfers between devices: 494 us -> none  [shards(): served = lax.all_gather(column, 'rep', axis=0, tiled=True)]
    ppermute x0 -> x3, waiting for transfers between devices: none -> 479 us  [turn_the_leaf(): lax.ppermute(new[0], axis_name=axis_id, perm=frames)]
    unnamed x6 -> x16, local copies, waits for them, and re-layouts: 21.5 us -> 53.5 us
    dynamic_slice x0 -> x1, local copies, waits for them, and re-layouts: none -> 20.2 us  [test_leaves_over_axis(): jnp.roll(jnp.concatenate(turn_the_leaf([matrix]), 0), (lax.axis_index(axi...]
  transfers between devices with their start and end apart: 1 -> 3, of which waited for: 1 -> 3; matrix products, arithmetic and copies ran while one was open for 0% -> 0% of each run, Pallas kernels for 0% -> 0%
where the time goes in v2:
time: 729 us; the launch traced here: 728 us
  waiting for transfers between devices  479 us (66%)
  local copies, waits for them, and re-layouts  122 us (17%)
  blocking collectives  92.8 us (13%)
  matrix products  31.7 us (4%)
    ppermute x3, waiting for transfers between devices, turn_the_leaf(): lax.ppermute(new[0], axis_name=axis_id, perm=frames)  479 us
    all_to_all x1, blocking collectives, shards(): lax.all_to_all(ordered, 'row', split_axis=1, concat_axis=0, tiled=True)  92.8 us
    unnamed x16, local copies, waits for them, and re-layouts  53.5 us
    dynamic_slice x1, local copies, waits for them, and re-layouts, test_leaves_over_axis(): jnp.roll(jnp.concatenate(turn_the_leaf([matrix]), 0), (lax.axis_index(axi...  20.2 us
    convert_element_type x1, local copies, waits for them, and re-layouts, shards(): ordered = picked.astype(jnp.bfloat16).reshape(rows_tile, cols_tile)  18.6 us
    dot_general x1, matrix products, shards(): jnp.einsum('ksj,rjkc->rskc', selector, tiled, preferred_element_type=jnp....  18.3 us
  transfers between devices with their start and end apart: 3, of which 3 were waited for; matrix products, arithmetic and copies ran while one was open for 0% of the time, Pallas kernels for 0%

profile of v2, /device:TPU:0, one launch (start us, length us, event | category | flops | bytes accessed | tf_op | source)
XLA Modules:
  0.0 727.7 jit_solution(16830019995929481203)
XLA Ops:
  0.6 0.0 copy-start
  0.7 0.8 dynamic-slice_bitcast_fusion
  1.5 0.1 copy.12
  1.6 12.8 %reshape.14 = bf16[896,2,4,512]{3,2,1,0:T(4,128)(2,1)} reshape(bf16[896,4096]{1,0:T(8,128)(2,1)} %param.4) | data formatting | bytes 14680064 | tf_op jit(solution)/shard_map/reshape | solution.py:36
  14.4 18.3 %fusion = bf16[896,2,4,512]{3,1,0,2:T(2,128)(2,1)} fusion(bf16[896,2,4,512]{3,2,1,0:T(4,128)(2,1)} %reshape.14, s32[4,2]{1,0:T(4,128)S(1)} %copy.12), kind=kOutput, calls=%fused_computation.1 | convolution fusion | flops 18350096 | bytes 14680096 | tf_op jit(solution)/shard_map/ksj,rjkc->rskc/dot_general | solution.py:37
  32.7 18.6 %copy.14 = bf16[896,2,4,512]{0,3,2,1:T(8,128)(2,1)} copy(bf16[896,2,4,512]{3,1,0,2:T(2,128)(2,1)} %fusion) | data formatting | bytes 14680064 | tf_op jit(solution)/shard_map/convert_element_type | solution.py:38
  51.3 92.8 %all_to_all.19 = bf16[896,2,2048]{0,2,1:T(8,128)(2,1)} all-to-all(bf16[896,2,2048]{0,2,1:T(8,128)(2,1)} %bitcast.21), channel_id=1, replica_groups=mesh['row'=2,'col'=4,'rep'=4] {'row'}, dimensions={1} | all-to-all | bytes 14680064 | tf_op jit(solution)/shard_map/all_to_all | solution.py:39
  144.2 11.3 %copy.15 = bf16[2,896,2048]{2,1,0:T(8,128)(2,1)} copy(bf16[2,896,2048]{1,2,0:T(8,128)(2,1)} %bitcast.22) | data formatting | bytes 14680064 | tf_op jit(solution)/shard_map/all_to_all | solution.py:39
  155.4 1.7 collective-permute-start
  157.2 159.4 %collective-permute-done = bf16[1792,2048]{1,0:T(8,128)(2,1)S(1)} collective-permute-done((bf16[1792,2048]{1,0:T(8,128)(2,1)}, bf16[1792,2048]{1,0:T(8,128)(2,1)S(1)}, u32[]{:S(2)}, u32[]{:S(2)}) %collective-permute-start) | collective-permute-done | bytes 7340064 | tf_op jit(solution)/shard_map/ppermute | solution.py:17
  316.6 0.0 copy-start.1
  316.6 3.0 copy-done.1
  319.6 0.0 collective-permute-start.1
  319.6 160.2 %collective-permute-done.1 = bf16[1792,2048]{1,0:T(8,128)(2,1)} collective-permute-done((bf16[1792,2048]{1,0:T(8,128)(2,1)S(1)}, bf16[1792,2048]{1,0:T(8,128)(2,1)}, u32[]{:S(2)}, u32[]{:S(2)}) %collective-permute-start.1) | collective-permute-done | bytes 7340064 | tf_op jit(solution)/shard_map/ppermute | solution.py:17
  479.8 0.0 collective-permute-start.2
  479.8 0.0 slice-start
  479.8 159.5 %collective-permute-done.2 = bf16[1792,2048]{1,0:T(8,128)(2,1)} collective-permute-done((bf16[1792,2048]{1,0:T(8,128)(2,1)}, bf16[1792,2048]{1,0:T(8,128)(2,1)}, u32[]{:S(2)}, u32[]{:S(2)}) %collective-permute-start.2) | collective-permute-done | bytes 7340064 | tf_op jit(solution)/shard_map/ppermute | solution.py:17
  639.3 7.4 %constant_dynamic-update-slice_fusion.7 = bf16[14336,2048]{1,0:T(8,128)(2,1)} fusion(bf16[1792,2048]{1,0:T(8,128)(2,1)} %collective-permute-done.2), kind=kLoop, calls=%fused_computation.11 | loop fusion | bytes 14680064
  646.7 0.0 slice-start.1
  646.7 7.6 %constant_dynamic-update-slice_fusion.6 = bf16[14336,2048]{1,0:T(8,128)(2,1)} fusion(bf16[14336,2048]{1,0:T(8,128)(2,1)} %constant_dynamic-update-slice_fusion.7, bf16[1792,2048]{1,0:T(8,128)(2,1)} %collective-permute-done.1), kind=kLoop, calls=%fused_computation.10 | loop fusion | bytes 14680064
  654.4 7.4 %constant_dynamic-update-slice_fusion.5 = bf16[14336,2048]{1,0:T(8,128)(2,1)} fusion(bf16[14336,2048]{1,0:T(8,128)(2,1)} %constant_dynamic-update-slice_fusion.6, bf16[1792,2048]{1,0:T(8,128)(2,1)} %copy-done.1), kind=kLoop, calls=%fused_computation.9 | loop fusion | bytes 14680064
  661.8 0.0 slice-done
  661.8 0.0 slice-done.1
  661.8 4.3 constant_dynamic-update-slice_fusion.4
  666.1 7.5 %constant_dynamic-update-slice_fusion.3 = bf16[14336,2048]{1,0:T(8,128)(2,1)} fusion(bf16[14336,2048]{1,0:T(8,128)(2,1)} %constant_dynamic-update-slice_fusion.4, bf16[1792,2048]{1,0:T(8,128)(2,1)} %collective-permute-done.2), kind=kLoop, calls=%fused_computation.7 | loop fusion | bytes 14680064
  673.6 7.5 %constant_dynamic-update-slice_fusion.2 = bf16[14336,2048]{1,0:T(8,128)(2,1)} fusion(bf16[14336,2048]{1,0:T(8,128)(2,1)} %constant_dynamic-update-slice_fusion.3, bf16[1792,2048]{1,0:T(8,128)(2,1)} %collective-permute-done.1), kind=kLoop, calls=%fused_computation.6 | loop fusion | bytes 14680064
  681.1 7.4 %constant_dynamic-update-slice_fusion.1 = bf16[14336,2048]{1,0:T(8,128)(2,1)} fusion(bf16[14336,2048]{1,0:T(8,128)(2,1)} %constant_dynamic-update-slice_fusion.2, bf16[1792,2048]{1,0:T(8,128)(2,1)} %copy-done.1), kind=kLoop, calls=%fused_computation.5 | loop fusion | bytes 14680064
  688.5 4.3 constant_dynamic-update-slice_fusion
  692.8 20.2 %constant_dynamic-slice_fusion = bf16[7168,2048]{1,0:T(8,128)(2,1)} fusion(bf16[14336,2048]{1,0:T(8,128)(2,1)} %constant_dynamic-update-slice_fusion, s32[]{:T(128)S(6)} %select_n.19), kind=kLoop, calls=%fused_computation.16 | loop fusion | bytes 58720260 | tf_op jit(solution)/shard_map/jit(_roll_dynamic)/dynamic_slice | solution.py:20
  713.0 0.0 copy-done
  713.0 13.3 %convolution_bitcast_fusion = f32[128,2048]{0,1:T(8,128)S(1)} fusion(bf16[7168,2048]{1,0:T(8,128)(2,1)} %constant_dynamic-slice_fusion, bf16[128,7168]{1,0:T(8,128)(2,1)S(1)} %copy-done), kind=kOutput, calls=%fused_computation.3 | convolution fusion | flops 3758096384 | bytes 32243712 | tf_op jit(solution)/shard_map/dot_general | solution.py:41
  726.4 1.3 copy.16
  (1 shorter events, 0.0 us)
Async XLA Ops:
  0.6 712.4 %copy-start = (bf16[128,7168]{1,0:T(8,128)(2,1)S(1)}, bf16[128,7168]{1,0:T(8,128)(2,1)}, u32[]{:S(2)}) copy-start(bf16[128,7168]{1,0:T(8,128)(2,1)} %param.3) | copy-start | bytes 5505028
  155.4 161.2 %collective-permute-start = (bf16[1792,2048]{1,0:T(8,128)(2,1)}, bf16[1792,2048]{1,0:T(8,128)(2,1)S(1)}, u32[]{:S(2)}, u32[]{:S(2)}) collective-permute-start(bf16[1792,2048]{1,0:T(8,128)(2,1)} %bitcast.16), channel_id=1, source_target_pairs={{0,1},{1,2},{2,3},{3,0},{4,5},{5,6},{6,7},{7,4},{8,9},{9,10},{10,1... | collective-permute-start | bytes 22020104 | tf_op jit(solution)/shard_map/ppermute | solution.py:17
  316.6 3.0 copy-start.1
  319.6 160.2 %collective-permute-start.1 = (bf16[1792,2048]{1,0:T(8,128)(2,1)S(1)}, bf16[1792,2048]{1,0:T(8,128)(2,1)}, u32[]{:S(2)}, u32[]{:S(2)}) collective-permute-start(bf16[1792,2048]{1,0:T(8,128)(2,1)S(1)} %collective-permute-done), channel_id=1, source_target_pairs={{0,1},{1,2},{2,3},{3,0},{4,5},{5,6},{6,7},{7,4},{8,9},{9,10},{10,1... | collective-permute-start | bytes 22020104 | tf_op jit(solution)/shard_map/ppermute | solution.py:17
  479.8 159.6 %collective-permute-start.2 = (bf16[1792,2048]{1,0:T(8,128)(2,1)}, bf16[1792,2048]{1,0:T(8,128)(2,1)}, u32[]{:S(2)}, u32[]{:S(2)}) collective-permute-start(bf16[1792,2048]{1,0:T(8,128)(2,1)} %collective-permute-done.1), channel_id=1, source_target_pairs={{0,1},{1,2},{2,3},{3,0},{4,5},{5,6},{6,7},{7,4},{8,9},{9,10},{10,1... | collective-permute-start | bytes 22020104 | tf_op jit(solution)/shard_map/ppermute | solution.py:17
  479.8 182.0 %slice-start = ((s8[7340032]{0:T(1024)(128)(4,1)}), s8[4194304]{0:T(1024)(128)(4,1)S(1)}, s32[]{:S(2)}) async-start(s8[7340032]{0:T(1024)(128)(4,1)} %bitcast.17), calls=%async_computation.1 | async-start | bytes 8388608
  646.7 15.0 %slice-start.1 = ((s8[7340032]{0:T(1024)(128)(4,1)}), s8[3145728]{0:T(1024)(128)(4,1)S(1)}, s32[]{:S(2)}) async-start(s8[7340032]{0:T(1024)(128)(4,1)} %bitcast.17), calls=%async_computation.2 | async-start | bytes 6291456
